TPU v7x, 32 devices: a whole 2x2x4 slice. The times are simulated.
32 devices in a mesh: dp: 8 (over y, x, core), seq: 4 (over z).
Axes of the slice: x: 2, y: 2, z: 4, core: 2. Of those that a mesh axis runs over, the one named last changes fastest.
Arguments:
- img_q_raw: bfloat16 [8, 512, 1536], P('dp', 'seq'), may hold values from -12 to 12
- img_k_raw: bfloat16 [8, 512, 1536], P('dp', 'seq'), may hold values from -6 to 6
- img_v: bfloat16 [8, 512, 1536], P('dp', 'seq'), may hold values from -6 to 6
- img_dout: bfloat16 [8, 512, 1536], P('dp', 'seq'), may hold values from -6 to 6
- txt_q_raw: bfloat16 [8, 64, 1536], P('dp', 'seq'), may hold values from -6 to 6
- txt_k_raw: bfloat16 [8, 64, 1536], P('dp'), may hold values from -6 to 6
- txt_v: bfloat16 [8, 64, 1536], P('dp'), may hold values from -6 to 6
- txt_dout: bfloat16 [8, 64, 1536], P('dp', 'seq'), may hold values from -6 to 6
- q_gain: float32 [128], replicated, may hold values from 0.6 to 3.8
- k_gain: float32 [128], replicated, may hold values from 0.6 to 3.8
Outputs:
- img_dq: bfloat16 [8, 512, 1536], P('dp', 'seq')
- img_dk: bfloat16 [8, 512, 1536], P('dp', 'seq')
- img_dv: bfloat16 [8, 512, 1536], P('dp', 'seq')
- txt_dq: bfloat16 [8, 64, 1536], P('dp', 'seq')
- txt_dk: bfloat16 [8, 64, 1536], P('dp', 'seq')
- txt_dv: bfloat16 [8, 64, 1536], P('dp', 'seq')
- q_gain_grad: float32 [128], replicated
- k_gain_grad: float32 [128], replicated
All inputs are finite; a program needn't handle non-finite values.
Results may differ from a plain program's by a relative error of at most 0.012.
The roundings to bfloat16 on the way count: a program that leaves them out, or rounds other values in their place, can miss the bound.
Values may be sent and summed in bfloat16 or wider, within the bound.
A program may use at most 64 MiB of HBM per device.

v0:
```python
import functools

import jax
import jax.numpy as jnp
from jax import lax
from jax.experimental import pallas as pl
from jax.experimental.pallas import tpu as pltpu
from jax.sharding import PartitionSpec as P

MESH = pl.DeviceIdType.MESH
HEAD_DIM = 128
EPSILON = 1e-06
F32 = jnp.float32
BF16 = jnp.bfloat16


def dot(a, b, contract):
    return lax.dot_general(a, b, ((contract[:1], contract[1:]), ((), ())), preferred_element_type=F32)


def inverse_rms(values):
    return lax.rsqrt(jnp.mean(values * values, axis=-1, keepdims=True) + EPSILON)


def norm_back(values, inverse, gain, upstream):
    unit = values * inverse
    lifted = upstream * gain
    mean = jnp.mean(lifted * unit, axis=-1, keepdims=True)
    return inverse * (lifted - unit * mean), upstream * unit


def partners(me, n):
    if n == 4:
        return [lax.rem(me + 2, n), 3 - me, me + 1 - 2 * lax.rem(me, 2)]
    return [lax.rem(me + step, n) for step in range(1, n)]


def kernel(
    n, dp, heads,
    h_iq, h_ik, h_iv, h_idt, h_tq, h_tk, h_tv, h_td, q_gain, k_gain,
    o_iq, o_ik, o_iv, o_tq, o_tk, o_tv, o_qg, o_kg,
    iq, ik, iv, idt, tq, tk, tv, td,
    qbuf, kbuf, vbuf, dbuf, knb, dka, dva, gq, gk, gv, gsum, dpbuf, sqbuf,
    fs, fr, bs, br, ls, gs, gr, ins,
):
    me = lax.axis_index("seq")
    my_dp = lax.axis_index("dp")
    img, txt, text = iq.shape[0], tq.shape[0], tk.shape[0]
    block = img + txt
    image = img * n
    others = partners(me, n)

    def col(owner, h):
        return pl.ds(pl.multiple_of((owner * heads + h) * HEAD_DIM, HEAD_DIM), HEAD_DIM)

    def rows(start, size, unit):
        return pl.ds(pl.multiple_of(start, unit), size)

    loads = [
        pltpu.make_async_copy(src, dst, ins.at[i])
        for i, (src, dst) in enumerate(
            zip(
                (h_iq, h_ik, h_iv, h_idt, h_tq, h_td, h_tk, h_tv),
                (iq, ik, iv, idt, tq, td, tk, tv),
            )
        )
    ]
    for load in loads:
        load.start()
    barrier = pltpu.get_barrier_semaphore()
    for other in others:
        pl.semaphore_signal(barrier, inc=1, device_id={"seq": other}, device_id_type=MESH)

    def greet(step, carry):
        pl.semaphore_signal(
            barrier, inc=1, device_id={"dp": lax.rem(my_dp + step, dp)}, device_id_type=MESH
        )
        return carry

    lax.fori_loop(1, dp, greet, 0)
    pl.semaphore_wait(barrier, n - 1 + dp - 1)
    for load in loads:
        load.wait()

    def forward_parts(h, source):
        return (
            (iq, qbuf.at[h, rows(source * block, img, 16)]),
            (ik, kbuf.at[h, rows(source * img, img, 16)]),
            (iv, vbuf.at[h, rows(source * img, img, 16)]),
            (idt, dbuf.at[h, rows(source * block, img, 16)]),
            (tq, qbuf.at[h, rows(source * block + img, txt, 16)]),
            (td, dbuf.at[h, rows(source * block + img, txt, 16)]),
        )

    def forward_copy(part, h, source, target):
        src, dst = forward_parts(h, source)[part]
        return pltpu.make_async_remote_copy(
            src_ref=src.at[:, col(target, h)], dst_ref=dst,
            send_sem=fs.at[part, h, target], recv_sem=fr.at[part, h, source],
            device_id={"seq": target}, device_id_type=MESH,
        )

    def send_head(h, carry):
        for other in others:
            for part in range(6):
                forward_copy(part, h, me, other).start()
        return carry

    lax.fori_loop(0, heads, send_head, 0)

    def own_head(h, carry):
        for src, dst in forward_parts(h, me):
            dst[...] = src[:, col(me, h)]
        kbuf[h, image:image + text] = tk[:, col(me, h)]
        vbuf[h, image:image + text] = tv[:, col(me, h)]
        return carry

    lax.fori_loop(0, heads, own_head, 0)
    gsum[...] = jnp.zeros_like(gsum)

    def back_parts(h, target):
        return (
            (gq.at[h, rows(target * block, img, 16)], o_iq),
            (gk.at[h, rows(target * img, img, 16)], o_ik),
            (gv.at[h, rows(target * img, img, 16)], o_iv),
            (gq.at[h, rows(target * block + img, txt, 16)], o_tq),
            (gk.at[h, rows(image + target * txt, txt, 16)], o_tk),
            (gv.at[h, rows(image + target * txt, txt, 16)], o_tv),
        )

    def back_copy(part, h, source, target):
        src, dst = back_parts(h, target)[part]
        return pltpu.make_async_remote_copy(
            src_ref=src, dst_ref=dst.at[:, col(source, h)],
            send_sem=bs.at[part, h, target], recv_sem=br.at[part, h, source],
            device_id={"seq": target}, device_id_type=MESH,
        )

    def send_back(h):
        for other in others:
            for part in range(6):
                back_copy(part, h, me, other).start()
        for part, (src, dst) in enumerate(back_parts(h, me)):
            pltpu.make_async_copy(src, dst.at[:, col(me, h)], ls.at[part, h]).start()

    qg = q_gain[...]
    kg = k_gain[...]
    scale = HEAD_DIM ** (-0.5)

    def head(h, carry):
        for other in others:
            for part in range(6):
                forward_copy(part, h, other, me).wait_recv()
        key_src = kbuf[h].astype(F32)
        key_inv = inverse_rms(key_src)
        knb[...] = (key_src * key_inv * kg).astype(BF16)
        dka[...] = jnp.zeros_like(dka)
        dva[...] = jnp.zeros_like(dva)

        def one_block(j, inner):
            here = rows(j * block, block, 16)
            query_src = qbuf[h, here].astype(F32)
            query_inv = inverse_rms(query_src)
            qn = (query_src * query_inv * qg).astype(BF16)
            kn = knb[...]
            value = vbuf[h]
            dout = dbuf[h, here]
            scores = dot(qn, kn, (1, 1)) * scale
            exps = jnp.exp(scores - jnp.max(scores, axis=-1, keepdims=True))
            prob = exps * (1.0 / jnp.sum(exps, axis=-1, keepdims=True))
            prob_b = prob.astype(BF16)
            output = dot(prob_b, value, (1, 0)).astype(BF16)
            dprob = dot(dout, value, (1, 1))
            delta = jnp.sum(dout.astype(F32) * output.astype(F32), axis=-1, keepdims=True)
            dscore = (prob * (dprob - delta) * scale).astype(BF16)
            dqn = dot(dscore, kn, (1, 0))
            dka[...] += dot(dscore, qn, (0, 0)).astype(BF16).astype(F32)
            dva[...] += dot(prob_b, dout, (0, 0)).astype(BF16).astype(F32)
            dq, term = norm_back(query_src, query_inv, qg, dqn)
            gq[h, here] = dq.astype(BF16)
            gsum[0:1, :] += jnp.sum(term, axis=0, keepdims=True)
            return inner

        lax.fori_loop(0, n, one_block, 0)
        gv[h] = dva[...].astype(BF16)
        dk, term = norm_back(key_src, key_inv, kg, dka[...])
        gk[h] = dk.astype(BF16)
        gsum[1:2, :] += jnp.sum(term, axis=0, keepdims=True)

        @pl.when(h < heads - 1)
        def _():
            send_back(h)

        return carry

    lax.fori_loop(0, heads, head, 0)

    dpbuf[my_dp] = gsum[...]

    def dp_copy(target):
        return pltpu.make_async_remote_copy(
            src_ref=dpbuf.at[my_dp], dst_ref=dpbuf.at[my_dp], send_sem=gs.at[0], recv_sem=gr.at[0],
            device_id={"dp": target}, device_id_type=MESH,
        )

    def dp_send(step, carry):
        dp_copy(lax.rem(my_dp + step, dp)).start()
        return carry

    lax.fori_loop(1, dp, dp_send, 0)
    rest = dpbuf.at[pl.ds(0, dp - 1)]
    pltpu.make_async_copy(rest, rest, gr.at[0]).wait()
    pltpu.make_async_copy(rest, rest, gs.at[0]).wait()
    sqbuf[me] = jnp.sum(dpbuf[...], axis=0)
    for other in others:
        pltpu.make_async_remote_copy(
            src_ref=sqbuf.at[me], dst_ref=sqbuf.at[me], send_sem=gs.at[1], recv_sem=gr.at[1],
            device_id={"seq": other}, device_id_type=MESH,
        ).start()
    send_back(heads - 1)

    def drain(h, carry):
        for part, (src, dst) in enumerate(back_parts(h, me)):
            pltpu.make_async_copy(src, dst.at[:, col(me, h)], ls.at[part, h]).wait()
        for other in others:
            for part in range(6):
                forward_copy(part, h, me, other).wait_send()
                back_copy(part, h, me, other).wait_send()
                back_copy(part, h, other, me).wait_recv()
        return carry

    lax.fori_loop(0, heads, drain, 0)
    rest = sqbuf.at[pl.ds(0, n - 1)]
    pltpu.make_async_copy(rest, rest, gr.at[1]).wait()
    pltpu.make_async_copy(rest, rest, gs.at[1]).wait()
    total = jnp.sum(sqbuf[...], axis=0)
    o_qg[...] = total[0:1]
    o_kg[...] = total[1:2]


def hand_on(*refs):
    count = (len(refs) - 2) // 3
    sources, results, held = refs[:count], refs[count:2 * count], refs[2 * count:3 * count]
    in_sem, out_sem = refs[3 * count:]
    loads = [pltpu.make_async_copy(a, b, in_sem.at[i]) for i, (a, b) in enumerate(zip(sources, held))]
    stores = [pltpu.make_async_copy(a, b, out_sem.at[i]) for i, (a, b) in enumerate(zip(held, results))]
    for load in loads:
        load.start()
    for load, store in zip(loads, stores):
        load.wait()
        store.start()
    for store in stores:
        store.wait()


def local(n, dp, iq, ik, iv, idt, tq, tk, tv, td, q_gain, k_gain):
    img, width = iq.shape[1:]
    txt, text = tq.shape[1], tk.shape[1]
    heads = width // HEAD_DIM // n
    keys = img * n + text
    queries = (img + txt) * n
    vmem = pl.BlockSpec(memory_space=pltpu.VMEM)
    hbm = pl.BlockSpec(memory_space=pl.ANY)
    out = pl.pallas_call(
        functools.partial(kernel, n, dp, heads),
        out_shape=(
            jax.ShapeDtypeStruct((img, width), BF16),
            jax.ShapeDtypeStruct((img, width), BF16),
            jax.ShapeDtypeStruct((img, width), BF16),
            jax.ShapeDtypeStruct((txt, width), BF16),
            jax.ShapeDtypeStruct((txt, width), BF16),
            jax.ShapeDtypeStruct((txt, width), BF16),
            jax.ShapeDtypeStruct((1, HEAD_DIM), F32),
            jax.ShapeDtypeStruct((1, HEAD_DIM), F32),
        ),
        in_specs=[hbm] * 8 + [vmem] * 2,
        out_specs=(hbm,) * 6 + (vmem,) * 2,
        scratch_shapes=[
            pltpu.VMEM((img, width), BF16),
            pltpu.VMEM((img, width), BF16),
            pltpu.VMEM((img, width), BF16),
            pltpu.VMEM((img, width), BF16),
            pltpu.VMEM((txt, width), BF16),
            pltpu.VMEM((text, width), BF16),
            pltpu.VMEM((text, width), BF16),
            pltpu.VMEM((txt, width), BF16),
            pltpu.VMEM((heads, queries, HEAD_DIM), BF16),
            pltpu.VMEM((heads, keys, HEAD_DIM), BF16),
            pltpu.VMEM((heads, keys, HEAD_DIM), BF16),
            pltpu.VMEM((heads, queries, HEAD_DIM), BF16),
            pltpu.VMEM((keys, HEAD_DIM), BF16),
            pltpu.VMEM((keys, HEAD_DIM), F32),
            pltpu.VMEM((keys, HEAD_DIM), F32),
            pltpu.VMEM((heads, queries, HEAD_DIM), BF16),
            pltpu.VMEM((heads, keys, HEAD_DIM), BF16),
            pltpu.VMEM((heads, keys, HEAD_DIM), BF16),
            pltpu.VMEM((2, HEAD_DIM), F32),
            pltpu.VMEM((dp, 2, HEAD_DIM), F32),
            pltpu.VMEM((n, 2, HEAD_DIM), F32),
            pltpu.SemaphoreType.DMA((6, heads, n)),
            pltpu.SemaphoreType.DMA((6, heads, n)),
            pltpu.SemaphoreType.DMA((6, heads, n)),
            pltpu.SemaphoreType.DMA((6, heads, n)),
            pltpu.SemaphoreType.DMA((6, heads)),
            pltpu.SemaphoreType.DMA((2,)),
            pltpu.SemaphoreType.DMA((2,)),
            pltpu.SemaphoreType.DMA((8,)),
        ],
        compiler_params=pltpu.CompilerParams(collective_id=0, has_side_effects=True),
    )(
        iq[0], ik[0], iv[0], idt[0], tq[0], tk[0], tv[0], td[0],
        q_gain.reshape(1, HEAD_DIM), k_gain.reshape(1, HEAD_DIM),
    )
    final = pl.pallas_call(
        hand_on,
        out_shape=tuple(jax.ShapeDtypeStruct(a.shape, a.dtype) for a in out),
        in_specs=[hbm] * 8,
        out_specs=(hbm,) * 8,
        scratch_shapes=[pltpu.VMEM(a.shape, a.dtype) for a in out]
        + [pltpu.SemaphoreType.DMA((8,)), pltpu.SemaphoreType.DMA((8,))],
    )(*out)
    return (*(grad[None] for grad in final[:6]), final[6][0], final[7][0])


def solution(mesh):
    split = P("dp", "seq", None)
    whole = P("dp", None, None)
    return jax.shard_map(
        functools.partial(local, mesh.shape["seq"], mesh.shape["dp"]),
        mesh=mesh,
        in_specs=(split, split, split, split, split, whole, whole, split, P(), P()),
        out_specs=(split,) * 6 + (P(), P()),
        check_vma=False,
    )
```

profile of v0, /device:TPU:8, one launch (start us, length us, event | category | flops | bytes accessed | tf_op | source)
XLA Modules:
  0.0 76.6 jit_solution(13131000317715789766)
XLA Ops:
  0.6 73.7 %shard_map.161 = (bf16[128,1536]{1,0:T(8,128)(2,1)}, bf16[128,1536]{1,0:T(8,128)(2,1)}, bf16[128,1536]{1,0:T(8,128)(2,1)}, bf16[16,1536]{1,0:T(8,128)(2,1)}, bf1...) custom-call(bf16[128,1536]{1,0:T(8,128)(2,1)} %bitcast.18, ...), custom_call_target="tpu_custom_call" | custom-call | tf_op jit(solution)/shard_map/pallas_call | solution.py:264
  74.4 2.2 %shard_map.162 = (bf16[128,1536]{1,0:T(8,128)(2,1)}, bf16[128,1536]{1,0:T(8,128)(2,1)}, bf16[128,1536]{1,0:T(8,128)(2,1)}, bf16[16,1536]{1,0:T(8,128)(2,1)}, bf1...) custom-call(bf16[128,1536]{1,0:T(8,128)(2,1)} %get-tuple-element.24.refs_0_, ...), custom_call_target="tpu_custom_call" | custom-call | tf_op jit(solution)/shard_map/pallas_call | solution.py:314
where the time goes:
time: 77.5 us; the launch traced here: 76.6 us
  Pallas kernels  75.9 us (98%)
    pallas_call x1, Pallas kernels, local(): pl.pallas_call(functools.partial(kernel, n, dp, heads), out_shape=(jax.Sh...  73.7 us
    pallas_call x1, Pallas kernels, local(): pl.pallas_call(hand_on, out_shape=tuple((jax.ShapeDtypeStruct(a.shape, a....  2.18 us

commit v1 on v0

v1 whole, which is shorter than its diff:
```python
import functools

import jax
import jax.numpy as jnp
from jax import lax
from jax.experimental import pallas as pl
from jax.experimental.pallas import tpu as pltpu
from jax.sharding import PartitionSpec as P

MESH = pl.DeviceIdType.MESH
HEAD_DIM = 128
EPSILON = 1e-06
VMEM_LIMIT = 24 * 1024 * 1024
F32 = jnp.float32
BF16 = jnp.bfloat16


def dot(a, b, contract):
    return lax.dot_general(a, b, ((contract[:1], contract[1:]), ((), ())), preferred_element_type=F32)


def inverse_rms(values):
    return lax.rsqrt(jnp.mean(values * values, axis=-1, keepdims=True) + EPSILON)


def norm_back(values, inverse, gain, upstream):
    unit = values * inverse
    lifted = upstream * gain
    mean = jnp.mean(lifted * unit, axis=-1, keepdims=True)
    return inverse * (lifted - unit * mean), upstream * unit


def ladder(dp):
    stages, stride = [], 1
    while stride < dp:
        radix = next(r for r in range(2, dp + 1) if (dp // stride) % r == 0)
        stages.append((stride, radix))
        stride *= radix
    return stages


def near_first(me, n, i):
    up = jnp.where(me + 1 + i < n, me + 1 + i, n - 2 - i)
    down = jnp.where(me - 1 - i >= 0, me - 1 - i, i + 1)
    return jnp.where(2 * me < n, up, down)


def far_first(me, n, i):
    up = jnp.where(n - 1 - i > me, n - 1 - i, n - 2 - i)
    down = jnp.where(i < me, i, i + 1)
    return jnp.where(2 * me < n, up, down)


def kernel(
    n, dp, heads,
    h_iq, h_ik, h_iv, h_idt, h_tq, h_tk, h_tv, h_td, h_qg, h_kg,
    y, total,
    x, tk, tv, gains, r, g, kc, vc, knb, dka, dva, gsum, dpbuf, sqbuf,
    ins, fs, fr, bs, br, gs, gr, tokens,
):
    me = lax.axis_index("seq")
    my_dp = lax.axis_index("dp")
    img, txt, text = h_iq.shape[0], h_tq.shape[0], h_tk.shape[0]
    block = img + txt
    sent = 2 * block + 2 * img
    back = 3 * block
    image = img * n
    stages = ladder(dp)
    has_left, has_right = me > 0, me < n - 1

    def col(owner, h):
        return pl.ds(pl.multiple_of((owner * heads + h) * HEAD_DIM, HEAD_DIM), HEAD_DIM)

    def rows(start, size):
        return pl.ds(pl.multiple_of(start, 16), size)

    def peers(stage):
        stride, radix = stages[stage]
        digit = lax.rem(lax.div(my_dp, stride), radix)
        return digit, [my_dp + (lax.rem(digit + s, radix) - digit) * stride for s in range(1, radix)]

    at = 0
    loads = []
    for src, size in ((h_iq, img), (h_tq, txt), (h_ik, img), (h_iv, img), (h_idt, img), (h_td, txt)):
        loads.append(pltpu.make_async_copy(src, x.at[pl.ds(at, size)], ins.at[0]))
        at += size
    loads.append(pltpu.make_async_copy(h_tk, tk, ins.at[1]))
    loads.append(pltpu.make_async_copy(h_tv, tv, ins.at[2]))
    loads.append(pltpu.make_async_copy(h_qg, gains.at[pl.ds(0, 1)], ins.at[3]))
    loads.append(pltpu.make_async_copy(h_kg, gains.at[pl.ds(1, 1)], ins.at[3]))
    barrier = pltpu.get_barrier_semaphore()

    @pl.when(has_left)
    def _():
        pl.semaphore_signal(barrier, inc=1, device_id={"seq": me - 1}, device_id_type=MESH)

    @pl.when(has_right)
    def _():
        pl.semaphore_signal(barrier, inc=1, device_id={"seq": me + 1}, device_id_type=MESH)

    greeted = 0
    for stage in range(len(stages)):
        for peer in peers(stage)[1]:
            pl.semaphore_signal(barrier, inc=1, device_id={"dp": peer}, device_id_type=MESH)
            greeted += 1
    for load in loads:
        load.start()
    pl.semaphore_wait(barrier, greeted + jnp.where(has_left, 1, 0) + jnp.where(has_right, 1, 0))

    def token(side, k, target):
        pl.semaphore_signal(tokens.at[side, k], inc=1, device_id={"seq": target}, device_id_type=MESH)

    @pl.when(has_left & has_right)
    def _():
        token(0, 0, me - 1)
        token(1, 0, me + 1)

    pltpu.make_async_copy(x, x, ins.at[0]).wait()

    def forward_copy(h, target):
        return pltpu.make_async_remote_copy(
            src_ref=x.at[:, col(target, h)], dst_ref=r.at[h, rows(me * sent, sent)],
            send_sem=fs.at[0], recv_sem=fr.at[h],
            device_id={"seq": target}, device_id_type=MESH,
        )

    first = near_first(me, n, 0)
    forward_copy(0, first).start()
    for k in range(n - 2):
        @pl.when(me < n - 2 - k)
        def _():
            pl.semaphore_wait(tokens.at[0, k], 1)

            @pl.when(has_left)
            def _():
                token(0, k + 1, me - 1)

        @pl.when(me > k + 1)
        def _():
            pl.semaphore_wait(tokens.at[1, k], 1)

            @pl.when(has_right)
            def _():
                token(1, k + 1, me + 1)

    for i in range(1, n - 1):
        forward_copy(0, near_first(me, n, i)).start()

    def send_head(h, carry):
        for i in range(n - 1):
            forward_copy(h, near_first(me, n, i)).start()
        return carry

    lax.fori_loop(1, heads, send_head, 0)

    def own_head(h, carry):
        r[h, rows(me * sent, sent)] = x[:, col(me, h)]
        return carry

    lax.fori_loop(0, heads, own_head, 0)
    gsum[...] = jnp.zeros_like(gsum)
    pltpu.make_async_copy(tk, tk, ins.at[1]).wait()
    pltpu.make_async_copy(tv, tv, ins.at[2]).wait()
    pltpu.make_async_copy(gains, gains, ins.at[3]).wait()

    def back_copy(h, target):
        return pltpu.make_async_remote_copy(
            src_ref=g.at[h, rows(target * back, back)], dst_ref=y.at[:, col(me, h)],
            send_sem=bs.at[0], recv_sem=br.at[0],
            device_id={"seq": target}, device_id_type=MESH,
        )

    def send_back(h):
        for i in range(n - 1):
            back_copy(h, far_first(me, n, i)).start()
        y[:, col(me, h)] = g[h, rows(me * back, back)]

    qg = gains[0:1]
    kg = gains[1:2]
    scale = HEAD_DIM ** (-0.5)

    def head(h, carry):
        rest = r.at[h, pl.ds(0, (n - 1) * sent)]
        pltpu.make_async_copy(rest, rest, fr.at[h]).wait()
        for j in range(n):
            kc[j * img:(j + 1) * img] = r[h, j * sent + block:j * sent + block + img]
            vc[j * img:(j + 1) * img] = r[h, j * sent + block + img:j * sent + block + 2 * img]
        kc[image:image + text] = tk[:, col(me, h)]
        vc[image:image + text] = tv[:, col(me, h)]
        key_src = kc[...].astype(F32)
        key_inv = inverse_rms(key_src)
        knb[...] = (key_src * key_inv * kg).astype(BF16)
        dka[...] = jnp.zeros_like(dka)
        dva[...] = jnp.zeros_like(dva)

        def one_block(j, inner):
            query_src = r[h, rows(j * sent, block)].astype(F32)
            query_inv = inverse_rms(query_src)
            qn = (query_src * query_inv * qg).astype(BF16)
            kn = knb[...]
            value = vc[...]
            dout = r[h, rows(j * sent + block + 2 * img, block)]
            scores = dot(qn, kn, (1, 1)) * scale
            exps = jnp.exp(scores - jnp.max(scores, axis=-1, keepdims=True))
            prob = exps * (1.0 / jnp.sum(exps, axis=-1, keepdims=True))
            prob_b = prob.astype(BF16)
            output = dot(prob_b, value, (1, 0)).astype(BF16)
            dprob = dot(dout, value, (1, 1))
            delta = jnp.sum(dout.astype(F32) * output.astype(F32), axis=-1, keepdims=True)
            dscore = (prob * (dprob - delta) * scale).astype(BF16)
            dqn = dot(dscore, kn, (1, 0))
            dka[...] += dot(dscore, qn, (0, 0)).astype(BF16).astype(F32)
            dva[...] += dot(prob_b, dout, (0, 0)).astype(BF16).astype(F32)
            dq, term = norm_back(query_src, query_inv, qg, dqn)
            g[h, rows(j * back, block)] = dq.astype(BF16)
            gsum[0:1, :] += jnp.sum(term, axis=0, keepdims=True)
            return inner

        lax.fori_loop(0, n, one_block, 0)
        dk, term = norm_back(key_src, key_inv, kg, dka[...])
        gsum[1:2, :] += jnp.sum(term, axis=0, keepdims=True)
        for part, grad in ((1, dk.astype(BF16)), (2, dva[...].astype(BF16))):
            for j in range(n):
                start = j * back + part * block
                g[h, start:start + img] = grad[j * img:(j + 1) * img]
                g[h, start + img:start + block] = grad[image + j * txt:image + (j + 1) * txt]

        @pl.when(h < heads - 1)
        def _():
            send_back(h)

        return carry

    lax.fori_loop(0, heads, head, 0)

    partial = gsum[...]
    base = 0
    for stage, (stride, radix) in enumerate(stages):
        digit, others = peers(stage)
        slot = dpbuf.at[base + digit]
        slot[...] = partial
        for peer in others:
            pltpu.make_async_remote_copy(
                src_ref=slot, dst_ref=slot, send_sem=gs.at[stage], recv_sem=gr.at[stage],
                device_id={"dp": peer}, device_id_type=MESH,
            ).start()
        rest = dpbuf.at[pl.ds(base, radix - 1)]
        pltpu.make_async_copy(rest, rest, gr.at[stage]).wait()
        partial = jnp.sum(dpbuf[base:base + radix], axis=0)
        base += radix
    last = len(stages)
    sqbuf[me] = partial
    for i in range(n - 1):
        pltpu.make_async_remote_copy(
            src_ref=sqbuf.at[me], dst_ref=sqbuf.at[me], send_sem=gs.at[last], recv_sem=gr.at[last],
            device_id={"seq": far_first(me, n, i)}, device_id_type=MESH,
        ).start()
    send_back(heads - 1)

    base = 0
    for stage, (stride, radix) in enumerate(stages):
        rest = dpbuf.at[pl.ds(base, radix - 1)]
        pltpu.make_async_copy(rest, rest, gs.at[stage]).wait()
        base += radix
    out = x.at[:, pl.ds(0, (n - 1) * heads * HEAD_DIM)]
    pltpu.make_async_copy(out, out, fs.at[0]).wait()
    rest = sqbuf.at[pl.ds(0, n - 1)]
    pltpu.make_async_copy(rest, rest, gr.at[last]).wait()
    pltpu.make_async_copy(rest, rest, gs.at[last]).wait()
    total[...] = jnp.sum(sqbuf[...], axis=0)
    out = y.at[:, pl.ds(0, (n - 1) * heads * HEAD_DIM)]
    pltpu.make_async_copy(out, out, bs.at[0]).wait()
    pltpu.make_async_copy(out, out, br.at[0]).wait()


def hand_on(y, total, *refs):
    grads, gains, sems = refs[:6], refs[6:8], refs[8]
    at = 0
    stores = []
    for out in grads:
        stores.append(pltpu.make_async_copy(y.at[pl.ds(at, out.shape[0])], out, sems.at[0]))
        at += out.shape[0]
    for i, out in enumerate(gains):
        stores.append(pltpu.make_async_copy(total.at[pl.ds(i, 1)], out, sems.at[1]))
    for store in stores:
        store.start()
    pltpu.make_async_copy(y, y, sems.at[0]).wait()
    pltpu.make_async_copy(total, total, sems.at[1]).wait()


def local(n, dp, iq, ik, iv, idt, tq, tk, tv, td, q_gain, k_gain):
    img, width = iq.shape[1:]
    txt, text = tq.shape[1], tk.shape[1]
    heads = width // HEAD_DIM // n
    keys = img * n + text
    block = img + txt
    sent, back = 2 * block + 2 * img, 3 * block
    stages = ladder(dp)
    vmem = pl.BlockSpec(memory_space=pltpu.VMEM)
    hbm = pl.BlockSpec(memory_space=pltpu.HBM)
    out = pl.pallas_call(
        functools.partial(kernel, n, dp, heads),
        out_shape=(
            jax.ShapeDtypeStruct((back, width), BF16),
            jax.ShapeDtypeStruct((2, HEAD_DIM), F32),
        ),
        in_specs=[hbm] * 10,
        out_specs=(vmem, vmem),
        scratch_shapes=[
            pltpu.VMEM((sent, width), BF16),
            pltpu.VMEM((text, width), BF16),
            pltpu.VMEM((text, width), BF16),
            pltpu.VMEM((2, HEAD_DIM), F32),
            pltpu.VMEM((heads, n * sent, HEAD_DIM), BF16),
            pltpu.VMEM((heads, n * back, HEAD_DIM), BF16),
            pltpu.VMEM((keys, HEAD_DIM), BF16),
            pltpu.VMEM((keys, HEAD_DIM), BF16),
            pltpu.VMEM((keys, HEAD_DIM), BF16),
            pltpu.VMEM((keys, HEAD_DIM), F32),
            pltpu.VMEM((keys, HEAD_DIM), F32),
            pltpu.VMEM((2, HEAD_DIM), F32),
            pltpu.VMEM((sum(radix for _, radix in stages), 2, HEAD_DIM), F32),
            pltpu.VMEM((n, 2, HEAD_DIM), F32),
            pltpu.SemaphoreType.DMA((4,)),
            pltpu.SemaphoreType.DMA((1,)),
            pltpu.SemaphoreType.DMA((heads,)),
            pltpu.SemaphoreType.DMA((1,)),
            pltpu.SemaphoreType.DMA((1,)),
            pltpu.SemaphoreType.DMA((len(stages) + 1,)),
            pltpu.SemaphoreType.DMA((len(stages) + 1,)),
            pltpu.SemaphoreType.REGULAR((2, max(n - 1, 1))),
        ],
        compiler_params=pltpu.CompilerParams(
            collective_id=0, has_side_effects=True, vmem_limit_bytes=VMEM_LIMIT
        ),
    )(
        *(pltpu.with_memory_space_constraint(a, pltpu.HBM) for a in (
        iq[0], ik[0], iv[0], idt[0], tq[0], tk[0], tv[0], td[0],
        q_gain.reshape(1, HEAD_DIM), k_gain.reshape(1, HEAD_DIM)))
    )
    image, rest = (img, width), (txt, width)
    final = pl.pallas_call(
        hand_on,
        out_shape=tuple(jax.ShapeDtypeStruct(a, BF16) for a in (image, rest) * 3)
        + (jax.ShapeDtypeStruct((1, HEAD_DIM), F32),) * 2,
        in_specs=[vmem] * 2,
        out_specs=(hbm,) * 8,
        scratch_shapes=[pltpu.SemaphoreType.DMA((2,))],
        compiler_params=pltpu.CompilerParams(vmem_limit_bytes=VMEM_LIMIT),
    )(*out)
    order = (0, 2, 4, 1, 3, 5)
    return (*(final[i][None] for i in order), final[6][0], final[7][0])


def solution(mesh):
    split = P("dp", "seq", None)
    whole = P("dp", None, None)
    return jax.shard_map(
        functools.partial(local, mesh.shape["seq"], mesh.shape["dp"]),
        mesh=mesh,
        in_specs=(split, split, split, split, split, whole, whole, split, P(), P()),
        out_specs=(split,) * 6 + (P(), P()),
        check_vma=False,
    )
```

time: 77.5 us -> 71.5 us (0.923)
  Pallas kernels: 75.9 us -> 70.2 us
    pallas_call x1, Pallas kernels: 73.7 us -> 69.1 us  [local(): pl.pallas_call(functools.partial(kernel, n, dp, heads), out_shape=(jax.Sh...]
    pallas_call x1, Pallas kernels: 2.18 us -> 1.06 us  [local(): pl.pallas_call(hand_on, out_shape=tuple((jax.ShapeDtypeStruct(a, BF16) fo...]
where the time goes in v1:
time: 71.5 us; the launch traced here: 70.8 us
  Pallas kernels  70.2 us (98%)
    pallas_call x1, Pallas kernels, local(): pl.pallas_call(functools.partial(kernel, n, dp, heads), out_shape=(jax.Sh...  69.1 us

profile of v1, /device:TPU:8, one launch (start us, length us, event | category | flops | bytes accessed | tf_op | source)
XLA Modules:
  0.0 70.8 jit_solution(4263668965325561986)
XLA Ops:
  0.6 69.1 %shard_map.161 = (bf16[432,1536]{1,0:T(8,128)(2,1)S(1)}, f32[2,128]{1,0:T(2,128)S(1)}) custom-call(bf16[128,1536]{1,0:T(8,128)(2,1)} %bitcast.18, bf16[128,1536]{1,0:T(8,128)(2,1)} %bitcast.19, bf16[128,1536]{1,0:T(8,128)(2,1)} %bitcast.20, bf16[128,1536]{1,0:T(8,128)(2,1)} %bitcast.21, bf16[16,1536]{1,0:T(8,128)(2,1)} %bitcast.24, ...), custom_call_target="tpu_custom_call" | custom-call | tf_op jit(solution)/shard_map/pallas_call | solution.py:301
  69.7 1.1 %shard_map.162 = (bf16[128,1536]{1,0:T(8,128)(2,1)}, bf16[16,1536]{1,0:T(8,128)(2,1)}, bf16[128,1536]{1,0:T(8,128)(2,1)}, bf16[16,1536]{1,0:T(8,128)(2,1)}, bf16...) custom-call(bf16[432,1536]{1,0:T(8,128)(2,1)S(1)} %get-tuple-element.18.y, ...), custom_call_target="tpu_custom_call" | custom-call | tf_op jit(solution)/shard_map/pallas_call | solution.py:342

commit v2 on v1

--- a/solution.py
+++ b/solution.py
@@ -56,7 +56,7 @@
     h_iq, h_ik, h_iv, h_idt, h_tq, h_tk, h_tv, h_td, h_qg, h_kg,
     y, total,
     x, tk, tv, gains, r, g, kc, vc, knb, dka, dva, gsum, dpbuf, sqbuf,
-    ins, fs, fr, bs, br, gs, gr, tokens,
+    ins, fs, fr, bs, br, gs, gr, tokens, column,
 ):
     me = lax.axis_index("seq")
     my_dp = lax.axis_index("dp")
@@ -79,43 +79,57 @@
         digit = lax.rem(lax.div(my_dp, stride), radix)
         return digit, [my_dp + (lax.rem(digit + s, radix) - digit) * stride for s in range(1, radix)]
 
-    at = 0
-    loads = []
-    for src, size in ((h_iq, img), (h_tq, txt), (h_ik, img), (h_iv, img), (h_idt, img), (h_td, txt)):
-        loads.append(pltpu.make_async_copy(src, x.at[pl.ds(at, size)], ins.at[0]))
-        at += size
-    loads.append(pltpu.make_async_copy(h_tk, tk, ins.at[1]))
-    loads.append(pltpu.make_async_copy(h_tv, tv, ins.at[2]))
-    loads.append(pltpu.make_async_copy(h_qg, gains.at[pl.ds(0, 1)], ins.at[3]))
-    loads.append(pltpu.make_async_copy(h_kg, gains.at[pl.ds(1, 1)], ins.at[3]))
+    order = [near_first(me, n, i) for i in range(n - 1)] + [me]
+
+    def band(i):
+        return pl.ds(pl.multiple_of(order[i] * heads * HEAD_DIM, HEAD_DIM), heads * HEAD_DIM)
+
+    def load_band(i):
+        at = 0
+        for src, size in ((h_iq, img), (h_tq, txt), (h_ik, img), (h_iv, img), (h_idt, img), (h_td, txt)):
+            pltpu.make_async_copy(
+                src.at[:, band(i)], x.at[pl.ds(at, size), band(i)], ins.at[i]
+            ).start()
+            at += size
+
+    def wait_band(i):
+        part = x.at[:, pl.ds(0, heads * HEAD_DIM)]
+        pltpu.make_async_copy(part, part, ins.at[i]).wait()
+
+    def small_loads():
+        return (
+            pltpu.make_async_copy(h_tk, tk, ins.at[n]),
+            pltpu.make_async_copy(h_tv, tv, ins.at[n + 1]),
+            pltpu.make_async_copy(h_qg, gains.at[pl.ds(0, 1)], ins.at[n + 2]),
+            pltpu.make_async_copy(h_kg, gains.at[pl.ds(1, 1)], ins.at[n + 2]),
+        )
+
     barrier = pltpu.get_barrier_semaphore()
 
+    def tell(ref, axis, target):
+        pl.semaphore_signal(ref, inc=1, device_id={axis: target}, device_id_type=MESH)
+
+    @pl.when(has_right)
+    def _():
+        tell(barrier, "seq", me + 1)
+
+    load_band(0)
+    dp_peers = [peer for stage in range(len(stages)) for peer in peers(stage)[1]]
+
+    @pl.when(me == 0)
+    def _():
+        for peer in dp_peers:
+            tell(barrier, "dp", peer)
+
+    for i in range(1, n):
+        load_band(i)
+    for load in small_loads():
+        load.start()
+
     @pl.when(has_left)
     def _():
-        pl.semaphore_signal(barrier, inc=1, device_id={"seq": me - 1}, device_id_type=MESH)
-
-    @pl.when(has_right)
-    def _():
-        pl.semaphore_signal(barrier, inc=1, device_id={"seq": me + 1}, device_id_type=MESH)
-
-    greeted = 0
-    for stage in range(len(stages)):
-        for peer in peers(stage)[1]:
-            pl.semaphore_signal(barrier, inc=1, device_id={"dp": peer}, device_id_type=MESH)
-            greeted += 1
-    for load in loads:
-        load.start()
-    pl.semaphore_wait(barrier, greeted + jnp.where(has_left, 1, 0) + jnp.where(has_right, 1, 0))
-
-    def token(side, k, target):
-        pl.semaphore_signal(tokens.at[side, k], inc=1, device_id={"seq": target}, device_id_type=MESH)
-
-    @pl.when(has_left & has_right)
-    def _():
-        token(0, 0, me - 1)
-        token(1, 0, me + 1)
-
-    pltpu.make_async_copy(x, x, ins.at[0]).wait()
+        pl.semaphore_wait(barrier, 1)
+        tell(tokens.at[0, 0], "seq", me - 1)
 
     def forward_copy(h, target):
         return pltpu.make_async_remote_copy(
@@ -124,34 +138,59 @@
             device_id={"seq": target}, device_id_type=MESH,
         )
 
-    first = near_first(me, n, 0)
-    forward_copy(0, first).start()
-    for k in range(n - 2):
-        @pl.when(me < n - 2 - k)
+    @pl.when(2 * me >= n)
+    def _():
+        wait_band(0)
+        forward_copy(0, order[0]).start()
+
+    for k in range(n - 1):
+        @pl.when(me < n - 1 - k)
         def _():
             pl.semaphore_wait(tokens.at[0, k], 1)
-
-            @pl.when(has_left)
-            def _():
-                token(0, k + 1, me - 1)
-
+            if k == 0:
+                @pl.when(2 * me < n)
+                def _():
+                    wait_band(0)
+                    forward_copy(0, order[0]).start()
+
+                @pl.when(has_left)
+                def _():
+                    tell(tokens.at[1, 0], "seq", me + 1)
+
+            if k < n - 2:
+                @pl.when(has_left)
+                def _():
+                    tell(tokens.at[0, k + 1], "seq", me - 1)
+
+    for k in range(n - 2):
         @pl.when(me > k + 1)
         def _():
             pl.semaphore_wait(tokens.at[1, k], 1)
-
-            @pl.when(has_right)
-            def _():
-                token(1, k + 1, me + 1)
+            if k < n - 3:
+                @pl.when(has_right)
+                def _():
+                    tell(tokens.at[1, k + 1], "seq", me + 1)
 
     for i in range(1, n - 1):
-        forward_copy(0, near_first(me, n, i)).start()
+        wait_band(i)
+        forward_copy(0, order[i]).start()
 
     def send_head(h, carry):
         for i in range(n - 1):
-            forward_copy(h, near_first(me, n, i)).start()
+            forward_copy(h, order[i]).start()
         return carry
 
     lax.fori_loop(1, heads, send_head, 0)
+    wait_band(n - 1)
+
+    @pl.when(me == 0)
+    def _():
+        pl.semaphore_wait(barrier, len(dp_peers))
+        for peer in dp_peers:
+            tell(column.at[0], "dp", peer)
+        pl.semaphore_wait(column.at[0], len(dp_peers))
+        for target in range(1, n):
+            tell(column.at[1], "seq", target)
 
     def own_head(h, carry):
         r[h, rows(me * sent, sent)] = x[:, col(me, h)]
@@ -159,9 +198,9 @@
 
     lax.fori_loop(0, heads, own_head, 0)
     gsum[...] = jnp.zeros_like(gsum)
-    pltpu.make_async_copy(tk, tk, ins.at[1]).wait()
-    pltpu.make_async_copy(tv, tv, ins.at[2]).wait()
-    pltpu.make_async_copy(gains, gains, ins.at[3]).wait()
+    pltpu.make_async_copy(tk, tk, ins.at[n]).wait()
+    pltpu.make_async_copy(tv, tv, ins.at[n + 1]).wait()
+    pltpu.make_async_copy(gains, gains, ins.at[n + 2]).wait()
 
     def back_copy(h, target):
         return pltpu.make_async_remote_copy(
@@ -173,6 +212,8 @@
     def send_back(h):
         for i in range(n - 1):
             back_copy(h, far_first(me, n, i)).start()
+
+    def keep_own(h):
         y[:, col(me, h)] = g[h, rows(me * back, back)]
 
     qg = gains[0:1]
@@ -229,9 +270,15 @@
         def _():
             send_back(h)
 
+        keep_own(h)
         return carry
 
     lax.fori_loop(0, heads, head, 0)
+
+
+    @pl.when(has_left)
+    def _():
+        pl.semaphore_wait(column.at[1], 1)
 
     partial = gsum[...]
     base = 0
@@ -255,7 +302,8 @@
             src_ref=sqbuf.at[me], dst_ref=sqbuf.at[me], send_sem=gs.at[last], recv_sem=gr.at[last],
             device_id={"seq": far_first(me, n, i)}, device_id_type=MESH,
         ).start()
-    send_back(heads - 1)
+    for i in range(n - 1):
+        back_copy(heads - 1, far_first(me, n, i)).start()
 
     base = 0
     for stage, (stride, radix) in enumerate(stages):
@@ -321,14 +369,15 @@
             pltpu.VMEM((2, HEAD_DIM), F32),
             pltpu.VMEM((sum(radix for _, radix in stages), 2, HEAD_DIM), F32),
             pltpu.VMEM((n, 2, HEAD_DIM), F32),
-            pltpu.SemaphoreType.DMA((4,)),
+            pltpu.SemaphoreType.DMA((n + 3,)),
             pltpu.SemaphoreType.DMA((1,)),
             pltpu.SemaphoreType.DMA((heads,)),
             pltpu.SemaphoreType.DMA((1,)),
             pltpu.SemaphoreType.DMA((1,)),
             pltpu.SemaphoreType.DMA((len(stages) + 1,)),
             pltpu.SemaphoreType.DMA((len(stages) + 1,)),
-            pltpu.SemaphoreType.REGULAR((2, max(n - 1, 1))),
+            pltpu.SemaphoreType.REGULAR((2, n)),
+            pltpu.SemaphoreType.REGULAR((2,)),
         ],
         compiler_params=pltpu.CompilerParams(
             collective_id=0, has_side_effects=True, vmem_limit_bytes=VMEM_LIMIT

time: 71.5 us -> 70.4 us (0.985)
  Pallas kernels: 70.2 us -> 69.1 us
    pallas_call x1, Pallas kernels: 69.1 us -> 68.1 us  [local(): pl.pallas_call(functools.partial(kernel, n, dp, heads), out_shape=(jax.Sh...]
where the time goes in v2:
time: 70.4 us; the launch traced here: 69.8 us
  Pallas kernels  69.1 us (98%)
    pallas_call x1, Pallas kernels, local(): pl.pallas_call(functools.partial(kernel, n, dp, heads), out_shape=(jax.Sh...  68.1 us

profile of v2, /device:TPU:8, one launch (start us, length us, event | category | flops | bytes accessed | tf_op | source)
XLA Modules:
  0.0 69.8 jit_solution(12897799317856817221)
XLA Ops:
  0.6 68.1 %shard_map.161 = (bf16[432,1536]{1,0:T(8,128)(2,1)S(1)}, f32[2,128]{1,0:T(2,128)S(1)}) custom-call(bf16[128,1536]{1,0:T(8,128)(2,1)} %bitcast.18, bf16[128,1536]{1,0:T(8,128)(2,1)} %bitcast.19, bf16[128,1536]{1,0:T(8,128)(2,1)} %bitcast.20, bf16[128,1536]{1,0:T(8,128)(2,1)} %bitcast.21, bf16[16,1536]{1,0:T(8,128)(2,1)} %bitcast.24, ...), custom_call_target="tpu_custom_call" | custom-call | tf_op jit(solution)/shard_map/pallas_call | solution.py:349
  68.7 1.1 %shard_map.162 = (bf16[128,1536]{1,0:T(8,128)(2,1)}, bf16[16,1536]{1,0:T(8,128)(2,1)}, bf16[128,1536]{1,0:T(8,128)(2,1)}, bf16[16,1536]{1,0:T(8,128)(2,1)}, bf16...) custom-call(bf16[432,1536]{1,0:T(8,128)(2,1)S(1)} %get-tuple-element.18.y, ...), custom_call_target="tpu_custom_call" | custom-call | tf_op jit(solution)/shard_map/pallas_call | solution.py:391

commit v3 on v2

--- a/solution.py
+++ b/solution.py
@@ -33,7 +33,8 @@
 def ladder(dp):
     stages, stride = [], 1
     while stride < dp:
-        radix = next(r for r in range(2, dp + 1) if (dp // stride) % r == 0)
+        left = dp // stride
+        radix = max((r for r in range(2, 9) if left % r == 0), default=left)
         stages.append((stride, radix))
         stride *= radix
     return stages
@@ -45,10 +46,12 @@
     return jnp.where(2 * me < n, up, down)
 
 
-def far_first(me, n, i):
-    up = jnp.where(n - 1 - i > me, n - 1 - i, n - 2 - i)
-    down = jnp.where(i < me, i, i + 1)
-    return jnp.where(2 * me < n, up, down)
+def cross_first(me, n, i):
+    half = n // 2
+    lower = me < half
+    count = jnp.where(lower, n - half, half)
+    own = jnp.where(lower, 0, half) + i - count
+    return jnp.where(i < count, jnp.where(lower, half, 0) + i, jnp.where(own < me, own, own + 1))
 
 
 def kernel(
@@ -86,15 +89,24 @@
 
     def load_band(i):
         at = 0
-        for src, size in ((h_iq, img), (h_tq, txt), (h_ik, img), (h_iv, img), (h_idt, img), (h_td, txt)):
-            pltpu.make_async_copy(
-                src.at[:, band(i)], x.at[pl.ds(at, size), band(i)], ins.at[i]
-            ).start()
+        for part, (src, size) in enumerate(
+            ((h_iq, img), (h_tq, txt), (h_ik, img), (h_iv, img), (h_idt, img), (h_td, txt))
+        ):
+            sem = ins.at[n + 3 if i == 0 and part == 0 else i]
+            pltpu.make_async_copy(src.at[:, band(i)], x.at[pl.ds(at, size), band(i)], sem).start()
             at += size
 
     def wait_band(i):
-        part = x.at[:, pl.ds(0, heads * HEAD_DIM)]
+        size = sent - img if i == 0 else sent
+        part = x.at[pl.ds(0, size), pl.ds(0, heads * HEAD_DIM)]
         pltpu.make_async_copy(part, part, ins.at[i]).wait()
+
+    def open_way():
+        part = x.at[pl.ds(0, img), pl.ds(0, heads * HEAD_DIM)]
+        pltpu.make_async_copy(part, part, ins.at[n + 3]).wait()
+        forward_piece(order[0], 0, img).start()
+        wait_band(0)
+        forward_piece(order[0], img, sent - img).start()
 
     def small_loads():
         return (
@@ -121,15 +133,24 @@
         for peer in dp_peers:
             tell(barrier, "dp", peer)
 
+    @pl.when(has_left)
+    def _():
+        pl.semaphore_wait(barrier, 1)
+        tell(tokens.at[0, 0], "seq", me - 1)
+
     for i in range(1, n):
         load_band(i)
     for load in small_loads():
         load.start()
 
-    @pl.when(has_left)
-    def _():
-        pl.semaphore_wait(barrier, 1)
-        tell(tokens.at[0, 0], "seq", me - 1)
+
+    def forward_piece(target, start, size):
+        return pltpu.make_async_remote_copy(
+            src_ref=x.at[pl.ds(start, size), col(target, 0)],
+            dst_ref=r.at[0, rows(me * sent + start, size)],
+            send_sem=fs.at[0], recv_sem=fr.at[0],
+            device_id={"seq": target}, device_id_type=MESH,
+        )
 
     def forward_copy(h, target):
         return pltpu.make_async_remote_copy(
@@ -140,8 +161,7 @@
 
     @pl.when(2 * me >= n)
     def _():
-        wait_band(0)
-        forward_copy(0, order[0]).start()
+        open_way()
 
     for k in range(n - 1):
         @pl.when(me < n - 1 - k)
@@ -150,8 +170,7 @@
             if k == 0:
                 @pl.when(2 * me < n)
                 def _():
-                    wait_band(0)
-                    forward_copy(0, order[0]).start()
+                    open_way()
 
                 @pl.when(has_left)
                 def _():
@@ -211,7 +230,9 @@
 
     def send_back(h):
         for i in range(n - 1):
-            back_copy(h, far_first(me, n, i)).start()
+            @pl.when((i != 1) | (h < heads - 2))
+            def _():
+                back_copy(h, cross_first(me, n, i)).start()
 
     def keep_own(h):
         y[:, col(me, h)] = g[h, rows(me * back, back)]
@@ -276,6 +297,8 @@
     lax.fori_loop(0, heads, head, 0)
 
 
+    back_copy(heads - 1, cross_first(me, n, 0)).start()
+
     @pl.when(has_left)
     def _():
         pl.semaphore_wait(column.at[1], 1)
@@ -300,10 +323,14 @@
     for i in range(n - 1):
         pltpu.make_async_remote_copy(
             src_ref=sqbuf.at[me], dst_ref=sqbuf.at[me], send_sem=gs.at[last], recv_sem=gr.at[last],
-            device_id={"seq": far_first(me, n, i)}, device_id_type=MESH,
+            device_id={"seq": cross_first(me, n, i)}, device_id_type=MESH,
         ).start()
-    for i in range(n - 1):
-        back_copy(heads - 1, far_first(me, n, i)).start()
+
+    if heads > 1 and n > 2:
+        back_copy(heads - 2, cross_first(me, n, 1)).start()
+
+    for i in range(1, n - 1):
+        back_copy(heads - 1, cross_first(me, n, i)).start()
 
     base = 0
     for stage, (stride, radix) in enumerate(stages):
@@ -369,7 +396,7 @@
             pltpu.VMEM((2, HEAD_DIM), F32),
             pltpu.VMEM((sum(radix for _, radix in stages), 2, HEAD_DIM), F32),
             pltpu.VMEM((n, 2, HEAD_DIM), F32),
-            pltpu.SemaphoreType.DMA((n + 3,)),
+            pltpu.SemaphoreType.DMA((n + 4,)),
             pltpu.SemaphoreType.DMA((1,)),
             pltpu.SemaphoreType.DMA((heads,)),
             pltpu.SemaphoreType.DMA((1,)),

time: 70.4 us -> 69.8 us (level)
  no operation moved by 1% of the time
where the time goes in v3:
time: 69.8 us; the launch traced here: 69.6 us
  Pallas kernels  69 us (99%)
    pallas_call x1, Pallas kernels, local(): pl.pallas_call(functools.partial(kernel, n, dp, heads), out_shape=(jax.Sh...  67.9 us

profile of v3, /device:TPU:8, one launch (start us, length us, event | category | flops | bytes accessed | tf_op | source)
XLA Modules:
  0.0 69.6 jit_solution(11289143735304487976)
XLA Ops:
  0.6 67.9 %shard_map.161 = (bf16[432,1536]{1,0:T(8,128)(2,1)S(1)}, f32[2,128]{1,0:T(2,128)S(1)}) custom-call(bf16[128,1536]{1,0:T(8,128)(2,1)} %bitcast.18, bf16[128,1536]{1,0:T(8,128)(2,1)} %bitcast.19, bf16[128,1536]{1,0:T(8,128)(2,1)} %bitcast.20, bf16[128,1536]{1,0:T(8,128)(2,1)} %bitcast.21, bf16[16,1536]{1,0:T(8,128)(2,1)} %bitcast.24, ...), custom_call_target="tpu_custom_call" | custom-call | tf_op jit(solution)/shard_map/pallas_call | solution.py:376
  68.6 1.1 %shard_map.162 = (bf16[128,1536]{1,0:T(8,128)(2,1)}, bf16[16,1536]{1,0:T(8,128)(2,1)}, bf16[128,1536]{1,0:T(8,128)(2,1)}, bf16[16,1536]{1,0:T(8,128)(2,1)}, bf16...) custom-call(bf16[432,1536]{1,0:T(8,128)(2,1)S(1)} %get-tuple-element.18.y, ...), custom_call_target="tpu_custom_call" | custom-call | tf_op jit(solution)/shard_map/pallas_call | solution.py:418

commit v4 on v3

--- a/solution.py
+++ b/solution.py
@@ -82,75 +82,30 @@
         digit = lax.rem(lax.div(my_dp, stride), radix)
         return digit, [my_dp + (lax.rem(digit + s, radix) - digit) * stride for s in range(1, radix)]
 
-    order = [near_first(me, n, i) for i in range(n - 1)] + [me]
-
-    def band(i):
-        return pl.ds(pl.multiple_of(order[i] * heads * HEAD_DIM, HEAD_DIM), heads * HEAD_DIM)
-
-    def load_band(i):
-        at = 0
-        for part, (src, size) in enumerate(
-            ((h_iq, img), (h_tq, txt), (h_ik, img), (h_iv, img), (h_idt, img), (h_td, txt))
-        ):
-            sem = ins.at[n + 3 if i == 0 and part == 0 else i]
-            pltpu.make_async_copy(src.at[:, band(i)], x.at[pl.ds(at, size), band(i)], sem).start()
-            at += size
-
-    def wait_band(i):
-        size = sent - img if i == 0 else sent
-        part = x.at[pl.ds(0, size), pl.ds(0, heads * HEAD_DIM)]
-        pltpu.make_async_copy(part, part, ins.at[i]).wait()
-
-    def open_way():
-        part = x.at[pl.ds(0, img), pl.ds(0, heads * HEAD_DIM)]
-        pltpu.make_async_copy(part, part, ins.at[n + 3]).wait()
-        forward_piece(order[0], 0, img).start()
-        wait_band(0)
-        forward_piece(order[0], img, sent - img).start()
-
-    def small_loads():
-        return (
-            pltpu.make_async_copy(h_tk, tk, ins.at[n]),
-            pltpu.make_async_copy(h_tv, tv, ins.at[n + 1]),
-            pltpu.make_async_copy(h_qg, gains.at[pl.ds(0, 1)], ins.at[n + 2]),
-            pltpu.make_async_copy(h_kg, gains.at[pl.ds(1, 1)], ins.at[n + 2]),
-        )
-
+    order = [near_first(me, n, i) for i in range(n - 1)]
+    parts, at = [], 0
+    for src, size in ((h_iq, img), (h_tq, txt), (h_ik, img), (h_iv, img), (h_idt, img), (h_td, txt)):
+        parts.append((src, at, size))
+        at += size
+    loads = [pltpu.make_async_copy(src, x.at[pl.ds(at, size)], ins.at[0]) for src, at, size in parts]
+    loads += [
+        pltpu.make_async_copy(h_tk, tk, ins.at[1]),
+        pltpu.make_async_copy(h_tv, tv, ins.at[2]),
+        pltpu.make_async_copy(h_qg, gains.at[pl.ds(0, 1)], ins.at[3]),
+        pltpu.make_async_copy(h_kg, gains.at[pl.ds(1, 1)], ins.at[3]),
+    ]
     barrier = pltpu.get_barrier_semaphore()
 
     def tell(ref, axis, target):
         pl.semaphore_signal(ref, inc=1, device_id={axis: target}, device_id_type=MESH)
 
-    @pl.when(has_right)
-    def _():
-        tell(barrier, "seq", me + 1)
-
-    load_band(0)
-    dp_peers = [peer for stage in range(len(stages)) for peer in peers(stage)[1]]
-
-    @pl.when(me == 0)
-    def _():
-        for peer in dp_peers:
-            tell(barrier, "dp", peer)
-
-    @pl.when(has_left)
-    def _():
-        pl.semaphore_wait(barrier, 1)
-        tell(tokens.at[0, 0], "seq", me - 1)
-
-    for i in range(1, n):
-        load_band(i)
-    for load in small_loads():
-        load.start()
-
-
-    def forward_piece(target, start, size):
-        return pltpu.make_async_remote_copy(
-            src_ref=x.at[pl.ds(start, size), col(target, 0)],
-            dst_ref=r.at[0, rows(me * sent + start, size)],
-            send_sem=fs.at[0], recv_sem=fr.at[0],
-            device_id={"seq": target}, device_id_type=MESH,
-        )
+    def first_copy():
+        for src, at, size in parts:
+            pltpu.make_async_remote_copy(
+                src_ref=src.at[:, col(order[0], 0)], dst_ref=r.at[0, rows(me * sent + at, size)],
+                send_sem=fs.at[0], recv_sem=fr.at[0],
+                device_id={"seq": order[0]}, device_id_type=MESH,
+            ).start()
 
     def forward_copy(h, target):
         return pltpu.make_async_remote_copy(
@@ -159,9 +114,27 @@
             device_id={"seq": target}, device_id_type=MESH,
         )
 
+    @pl.when(has_right)
+    def _():
+        tell(barrier, "seq", me + 1)
+
+    @pl.when(has_left)
+    def _():
+        pl.semaphore_wait(barrier, 1)
+        tell(tokens.at[0, 0], "seq", me - 1)
+
     @pl.when(2 * me >= n)
     def _():
-        open_way()
+        first_copy()
+
+    for load in loads:
+        load.start()
+    dp_peers = [peer for stage in range(len(stages)) for peer in peers(stage)[1]]
+
+    @pl.when(me == 0)
+    def _():
+        for peer in dp_peers:
+            tell(barrier, "dp", peer)
 
     for k in range(n - 1):
         @pl.when(me < n - 1 - k)
@@ -170,7 +143,7 @@
             if k == 0:
                 @pl.when(2 * me < n)
                 def _():
-                    open_way()
+                    first_copy()
 
                 @pl.when(has_left)
                 def _():
@@ -190,8 +163,8 @@
                 def _():
                     tell(tokens.at[1, k + 1], "seq", me + 1)
 
+    pltpu.make_async_copy(x, x, ins.at[0]).wait()
     for i in range(1, n - 1):
-        wait_band(i)
         forward_copy(0, order[i]).start()
 
     def send_head(h, carry):
@@ -200,7 +173,6 @@
         return carry
 
     lax.fori_loop(1, heads, send_head, 0)
-    wait_band(n - 1)
 
     @pl.when(me == 0)
     def _():
@@ -217,9 +189,9 @@
 
     lax.fori_loop(0, heads, own_head, 0)
     gsum[...] = jnp.zeros_like(gsum)
-    pltpu.make_async_copy(tk, tk, ins.at[n]).wait()
-    pltpu.make_async_copy(tv, tv, ins.at[n + 1]).wait()
-    pltpu.make_async_copy(gains, gains, ins.at[n + 2]).wait()
+    pltpu.make_async_copy(tk, tk, ins.at[1]).wait()
+    pltpu.make_async_copy(tv, tv, ins.at[2]).wait()
+    pltpu.make_async_copy(gains, gains, ins.at[3]).wait()
 
     def back_copy(h, target):
         return pltpu.make_async_remote_copy(
@@ -396,7 +368,7 @@
             pltpu.VMEM((2, HEAD_DIM), F32),
             pltpu.VMEM((sum(radix for _, radix in stages), 2, HEAD_DIM), F32),
             pltpu.VMEM((n, 2, HEAD_DIM), F32),
-            pltpu.SemaphoreType.DMA((n + 4,)),
+            pltpu.SemaphoreType.DMA((4,)),
             pltpu.SemaphoreType.DMA((1,)),
             pltpu.SemaphoreType.DMA((heads,)),
             pltpu.SemaphoreType.DMA((1,)),

time: 69.8 us -> 69.2 us (level)
  no operation moved by 1% of the time
where the time goes in v4:
time: 69.2 us; the launch traced here: 69.1 us
  Pallas kernels  68.4 us (99%)
    pallas_call x1, Pallas kernels, local(): pl.pallas_call(functools.partial(kernel, n, dp, heads), out_shape=(jax.Sh...  67.4 us

profile of v4, /device:TPU:8, one launch (start us, length us, event | category | flops | bytes accessed | tf_op | source)
XLA Modules:
  0.0 69.1 jit_solution(7683513296549161096)
XLA Ops:
  0.6 67.4 %shard_map.161 = (bf16[432,1536]{1,0:T(8,128)(2,1)S(1)}, f32[2,128]{1,0:T(2,128)S(1)}) custom-call(bf16[128,1536]{1,0:T(8,128)(2,1)} %bitcast.18, bf16[128,1536]{1,0:T(8,128)(2,1)} %bitcast.19, bf16[128,1536]{1,0:T(8,128)(2,1)} %bitcast.20, bf16[128,1536]{1,0:T(8,128)(2,1)} %bitcast.21, bf16[16,1536]{1,0:T(8,128)(2,1)} %bitcast.24, ...), custom_call_target="tpu_custom_call" | custom-call | tf_op jit(solution)/shard_map/pallas_call | solution.py:348
  68.0 1.1 %shard_map.162 = (bf16[128,1536]{1,0:T(8,128)(2,1)}, bf16[16,1536]{1,0:T(8,128)(2,1)}, bf16[128,1536]{1,0:T(8,128)(2,1)}, bf16[16,1536]{1,0:T(8,128)(2,1)}, bf16...) custom-call(bf16[432,1536]{1,0:T(8,128)(2,1)S(1)} %get-tuple-element.18.y, ...), custom_call_target="tpu_custom_call" | custom-call | tf_op jit(solution)/shard_map/pallas_call | solution.py:390

commit v5 on v4

--- a/solution.py
+++ b/solution.py
@@ -58,7 +58,7 @@
     n, dp, heads,
     h_iq, h_ik, h_iv, h_idt, h_tq, h_tk, h_tv, h_td, h_qg, h_kg,
     y, total,
-    x, tk, tv, gains, r, g, kc, vc, knb, dka, dva, gsum, dpbuf, sqbuf,
+    x, gains, r, g, kc, vc, knb, dka, dva, gsum, dpbuf, sqbuf,
     ins, fs, fr, bs, br, gs, gr, tokens, column,
 ):
     me = lax.axis_index("seq")
@@ -89,10 +89,10 @@
         at += size
     loads = [pltpu.make_async_copy(src, x.at[pl.ds(at, size)], ins.at[0]) for src, at, size in parts]
     loads += [
-        pltpu.make_async_copy(h_tk, tk, ins.at[1]),
-        pltpu.make_async_copy(h_tv, tv, ins.at[2]),
-        pltpu.make_async_copy(h_qg, gains.at[pl.ds(0, 1)], ins.at[3]),
-        pltpu.make_async_copy(h_kg, gains.at[pl.ds(1, 1)], ins.at[3]),
+        pltpu.make_async_copy(h_tk, x.at[pl.ds(sent, text)], ins.at[0]),
+        pltpu.make_async_copy(h_tv, x.at[pl.ds(sent + text, text)], ins.at[0]),
+        pltpu.make_async_copy(h_qg, gains.at[pl.ds(0, 1)], ins.at[1]),
+        pltpu.make_async_copy(h_kg, gains.at[pl.ds(1, 1)], ins.at[1]),
     ]
     barrier = pltpu.get_barrier_semaphore()
 
@@ -109,19 +109,28 @@
 
     def forward_copy(h, target):
         return pltpu.make_async_remote_copy(
-            src_ref=x.at[:, col(target, h)], dst_ref=r.at[h, rows(me * sent, sent)],
+            src_ref=x.at[pl.ds(0, sent), col(target, h)], dst_ref=r.at[h, rows(me * sent, sent)],
             send_sem=fs.at[0], recv_sem=fr.at[h],
             device_id={"seq": target}, device_id_type=MESH,
         )
 
+    middle = n // 2 if n > 3 else n
+
+    @pl.when(me == middle)
+    def _():
+        tell(barrier, "seq", me - 1)
+
     @pl.when(has_right)
     def _():
         tell(barrier, "seq", me + 1)
 
     @pl.when(has_left)
     def _():
-        pl.semaphore_wait(barrier, 1)
-        tell(tokens.at[0, 0], "seq", me - 1)
+        pl.semaphore_wait(barrier, jnp.where(me == middle - 1, 2, 1))
+
+    @pl.when(has_left & (me != middle))
+    def _():
+        tell(tokens.at[0], "seq", me - 1)
 
     @pl.when(2 * me >= n)
     def _():
@@ -139,7 +148,12 @@
     for k in range(n - 1):
         @pl.when(me < n - 1 - k)
         def _():
-            pl.semaphore_wait(tokens.at[0, k], 1)
+            if k == 0:
+                @pl.when(me != middle - 1)
+                def _():
+                    pl.semaphore_wait(tokens.at[0], 1)
+            else:
+                pl.semaphore_wait(tokens.at[k], 1)
             if k == 0:
                 @pl.when(2 * me < n)
                 def _():
@@ -147,21 +161,21 @@
 
                 @pl.when(has_left)
                 def _():
-                    tell(tokens.at[1, 0], "seq", me + 1)
+                    tell(tokens.at[n - 1], "seq", me + 1)
 
             if k < n - 2:
                 @pl.when(has_left)
                 def _():
-                    tell(tokens.at[0, k + 1], "seq", me - 1)
+                    tell(tokens.at[k + 1], "seq", me - 1)
 
     for k in range(n - 2):
         @pl.when(me > k + 1)
         def _():
-            pl.semaphore_wait(tokens.at[1, k], 1)
+            pl.semaphore_wait(tokens.at[n - 1 + k], 1)
             if k < n - 3:
                 @pl.when(has_right)
                 def _():
-                    tell(tokens.at[1, k + 1], "seq", me + 1)
+                    tell(tokens.at[n + k], "seq", me + 1)
 
     pltpu.make_async_copy(x, x, ins.at[0]).wait()
     for i in range(1, n - 1):
@@ -184,14 +198,12 @@
             tell(column.at[1], "seq", target)
 
     def own_head(h, carry):
-        r[h, rows(me * sent, sent)] = x[:, col(me, h)]
+        r[h, rows(me * sent, sent)] = x[0:sent, col(me, h)]
         return carry
 
     lax.fori_loop(0, heads, own_head, 0)
     gsum[...] = jnp.zeros_like(gsum)
-    pltpu.make_async_copy(tk, tk, ins.at[1]).wait()
-    pltpu.make_async_copy(tv, tv, ins.at[2]).wait()
-    pltpu.make_async_copy(gains, gains, ins.at[3]).wait()
+    pltpu.make_async_copy(gains, gains, ins.at[1]).wait()
 
     def back_copy(h, target):
         return pltpu.make_async_remote_copy(
@@ -200,9 +212,11 @@
             device_id={"seq": target}, device_id_type=MESH,
         )
 
+    keep = (me == n - 1)
+
     def send_back(h):
         for i in range(n - 1):
-            @pl.when((i != 1) | (h < heads - 2))
+            @pl.when((i != 1) | (h < heads - 2) | keep)
             def _():
                 back_copy(h, cross_first(me, n, i)).start()
 
@@ -219,8 +233,8 @@
         for j in range(n):
             kc[j * img:(j + 1) * img] = r[h, j * sent + block:j * sent + block + img]
             vc[j * img:(j + 1) * img] = r[h, j * sent + block + img:j * sent + block + 2 * img]
-        kc[image:image + text] = tk[:, col(me, h)]
-        vc[image:image + text] = tv[:, col(me, h)]
+        kc[image:image + text] = x[sent:sent + text, col(me, h)]
+        vc[image:image + text] = x[sent + text:sent + 2 * text, col(me, h)]
         key_src = kc[...].astype(F32)
         key_inv = inverse_rms(key_src)
         knb[...] = (key_src * key_inv * kg).astype(BF16)
@@ -299,7 +313,9 @@
         ).start()
 
     if heads > 1 and n > 2:
-        back_copy(heads - 2, cross_first(me, n, 1)).start()
+        @pl.when(jnp.logical_not(keep))
+        def _():
+            back_copy(heads - 2, cross_first(me, n, 1)).start()
 
     for i in range(1, n - 1):
         back_copy(heads - 1, cross_first(me, n, i)).start()
@@ -309,7 +325,7 @@
         rest = dpbuf.at[pl.ds(base, radix - 1)]
         pltpu.make_async_copy(rest, rest, gs.at[stage]).wait()
         base += radix
-    out = x.at[:, pl.ds(0, (n - 1) * heads * HEAD_DIM)]
+    out = x.at[pl.ds(0, sent), pl.ds(0, (n - 1) * heads * HEAD_DIM)]
     pltpu.make_async_copy(out, out, fs.at[0]).wait()
     rest = sqbuf.at[pl.ds(0, n - 1)]
     pltpu.make_async_copy(rest, rest, gr.at[last]).wait()
@@ -354,9 +370,7 @@
         in_specs=[hbm] * 10,
         out_specs=(vmem, vmem),
         scratch_shapes=[
-            pltpu.VMEM((sent, width), BF16),
-            pltpu.VMEM((text, width), BF16),
-            pltpu.VMEM((text, width), BF16),
+            pltpu.VMEM((sent + 2 * text, width), BF16),
             pltpu.VMEM((2, HEAD_DIM), F32),
             pltpu.VMEM((heads, n * sent, HEAD_DIM), BF16),
             pltpu.VMEM((heads, n * back, HEAD_DIM), BF16),
@@ -368,14 +382,14 @@
             pltpu.VMEM((2, HEAD_DIM), F32),
             pltpu.VMEM((sum(radix for _, radix in stages), 2, HEAD_DIM), F32),
             pltpu.VMEM((n, 2, HEAD_DIM), F32),
-            pltpu.SemaphoreType.DMA((4,)),
+            pltpu.SemaphoreType.DMA((2,)),
             pltpu.SemaphoreType.DMA((1,)),
             pltpu.SemaphoreType.DMA((heads,)),
             pltpu.SemaphoreType.DMA((1,)),
             pltpu.SemaphoreType.DMA((1,)),
             pltpu.SemaphoreType.DMA((len(stages) + 1,)),
             pltpu.SemaphoreType.DMA((len(stages) + 1,)),
-            pltpu.SemaphoreType.REGULAR((2, n)),
+            pltpu.SemaphoreType.REGULAR((2 * n - 3,)),
             pltpu.SemaphoreType.REGULAR((2,)),
         ],
         compiler_params=pltpu.CompilerParams(

time: 69.2 us -> 69.1 us (level)
  no operation moved by 1% of the time
where the time goes in v5:
time: 69.1 us; the launch traced here: 69 us
  Pallas kernels  68.3 us (99%)
    pallas_call x1, Pallas kernels, local(): pl.pallas_call(functools.partial(kernel, n, dp, heads), out_shape=(jax.Sh...  67.3 us

profile of v5, /device:TPU:8, one launch (start us, length us, event | category | flops | bytes accessed | tf_op | source)
XLA Modules:
  0.0 69.0 jit_solution(2686649067902172906)
XLA Ops:
  0.6 67.3 %shard_map.161 = (bf16[432,1536]{1,0:T(8,128)(2,1)S(1)}, f32[2,128]{1,0:T(2,128)S(1)}) custom-call(bf16[128,1536]{1,0:T(8,128)(2,1)} %bitcast.18, bf16[128,1536]{1,0:T(8,128)(2,1)} %bitcast.19, bf16[128,1536]{1,0:T(8,128)(2,1)} %bitcast.20, bf16[128,1536]{1,0:T(8,128)(2,1)} %bitcast.21, bf16[16,1536]{1,0:T(8,128)(2,1)} %bitcast.24, ...), custom_call_target="tpu_custom_call" | custom-call | tf_op jit(solution)/shard_map/pallas_call | solution.py:364
  67.9 1.1 %shard_map.162 = (bf16[128,1536]{1,0:T(8,128)(2,1)}, bf16[16,1536]{1,0:T(8,128)(2,1)}, bf16[128,1536]{1,0:T(8,128)(2,1)}, bf16[16,1536]{1,0:T(8,128)(2,1)}, bf16...) custom-call(bf16[432,1536]{1,0:T(8,128)(2,1)S(1)} %get-tuple-element.18.y, ...), custom_call_target="tpu_custom_call" | custom-call | tf_op jit(solution)/shard_map/pallas_call | solution.py:404
